TPU v7x, 32 devices: a whole 2x2x4 slice. The times are simulated.
32 devices in a mesh: dp: 8 (over z, x), owner: 4 (over y, core).
Axes of the slice: x: 2, y: 2, z: 4, core: 2. Of those that a mesh axis runs over, the one named last changes fastest.
Arguments:
- gradients: float32 [8, 1024, 7168], P(None, 'dp', 'owner'), may hold values from -6 to 6
- rows_live: int32 [8], replicated, may hold values from 256 to 1024
Outputs:
- updates: bfloat16 [8, 1024, 7168], P(None, 'dp', 'owner')
All inputs are finite; a program needn't handle non-finite values.
Results may differ from a plain program's by a relative error of at most 0.015.
Values may be sent and summed in bfloat16 or wider, within the bound.
A program may use at most 64 MiB of HBM per device.

v0:
```python
import math

import jax
import jax.numpy as jnp
from jax import lax
from jax.sharding import PartitionSpec as P

D = 7168


def body(gradients, rows_live):
    narrowed = gradients.astype(jnp.bfloat16)
    regrouped = lax.all_to_all(narrowed, "dp", split_axis=0, concat_axis=1, tiled=True)
    owned_count = regrouped.shape[0]
    hidden_rows = regrouped.shape[1]
    first_owned = lax.axis_index("dp") * owned_count
    live_counts = lax.dynamic_slice_in_dim(rows_live, first_owned, owned_count)
    live_mask = jnp.arange(hidden_rows, dtype=jnp.int32)[None, :, None] < live_counts[:, None, None]
    regrouped = jnp.where(live_mask, regrouped, jnp.zeros_like(regrouped))
    partial_gram = jnp.einsum(
        "mcr,mdr->mcd", regrouped, regrouped, preferred_element_type=jnp.float32
    )
    live_float = live_counts.astype(jnp.float32)
    whole_gram = lax.psum(partial_gram.astype(jnp.bfloat16), "owner").astype(jnp.float32)
    trace_total = jnp.trace(whole_gram, axis1=1, axis2=2)
    scale_sq = 2.0 * trace_total / live_float
    normed_gram = (whole_gram / scale_sq[:, None, None]).astype(jnp.bfloat16)
    inverse = (1.0 / jnp.sqrt(scale_sq))[:, None, None]
    once = (
        jnp.einsum("mcd,mdr->mcr", normed_gram, regrouped, preferred_element_type=jnp.float32)
        * inverse
    )
    twice = jnp.einsum(
        "mcd,mdr->mcr", normed_gram, once.astype(jnp.bfloat16), preferred_element_type=jnp.float32
    )
    combined = 3.4445 * regrouped.astype(jnp.float32) * inverse - 4.775 * once + 2.0315 * twice
    update_rows = (combined * (0.2 * math.sqrt(D))).astype(jnp.bfloat16)
    return lax.all_to_all(update_rows, "dp", split_axis=1, concat_axis=0, tiled=True)


def solution(mesh):
    return jax.shard_map(
        body,
        mesh=mesh,
        in_specs=(P(None, "dp", "owner"), P()),
        out_specs=P(None, "dp", "owner"),
        check_vma=False,
    )
```

profile of v0, /device:TPU:17, one launch (start us, length us, event | category | flops | bytes accessed | tf_op | source)
XLA Modules:
  0.0 385.8 jit_solution(16820926485267107496)
XLA Ops:
  6.5 5.3 %convert_element_type.32 = bf16[8,128,1792]{2,1,0:T(8,128)(2,1)} convert(f32[8,128,1792]{2,1,0:T(8,128)} %param.2) | non-fusion elementwise | flops 1835008 | bytes 11010048 | tf_op jit(solution)/shard_map/convert_element_type | solution.py:12
  11.9 5.7 %all-to-all-start = ((bf16[8,128,1792]{2,1,0:T(8,128)(2,1)}), bf16[8,128,1792]{2,1,0:T(8,128)(2,1)}, u32[]{:S(2)}, u32[]{:S(2)}) async-start(bf16[8,128,1792]{2,1,0:T(8,128)(2,1)} %convert_element_type.32), calls=%async_computation | async-start | bytes 7340032 | tf_op jit(solution)/shard_map/all_to_all | solution.py:13
  17.6 0.0 all-reduce.2.cloned.1.call-start
  17.6 0.0 copy-done.2
  17.6 0.6 dynamic_slice.3
  18.2 0.6 iota_compare_fusion.1
  18.8 76.9 %all-to-all-done = bf16[8,128,1792]{2,1,0:T(8,128)(2,1)} async-done(((bf16[8,128,1792]{2,1,0:T(8,128)(2,1)}), bf16[8,128,1792]{2,1,0:T(8,128)(2,1)}, u32[]{:S(2)}, u32[]{:S(2)}) %all-to-all-start) | async-done | bytes 3670048 | tf_op jit(solution)/shard_map/all_to_all | solution.py:13
  95.7 8.6 %convert_bitcast_fusion = bf16[1,1024,1024]{2,1,0:T(8,128)(2,1)} fusion(bf16[1,1024,1,1,1,1,1792]{6,1,5,4,3,2,0:T(8,128)(2,1)} %bitcast.2, pred[1024]{0:T(1024)(128)(4,1)S(1)} %iota_compare_fusion.1), kind=kOutput, calls=%fused_computation.16 | convolution fusion | flops 3760979968 | bytes 5768192 | tf_op jit(solution)/shard_map/mcr,mdr->mcd/dot_general | solution.py:20
  104.3 0.0 all-reduce.2.cloned.1.call-update
  104.9 4.2 %bitcast_select_fusion = bf16[1024,1792]{1,0:T(8,128)(2,1)} fusion(bf16[8,128,1792]{2,1,0:T(8,128)(2,1)} %all-to-all-done, pred[1024]{0:T(1024)(128)(4,1)S(1)} %iota_compare_fusion.1), kind=kLoop, calls=%fused_computation.11 | loop fusion | flops 1835008 | bytes 7341056 | tf_op jit(solution)/shard_map/jit(_where)/select_n | solution.py:19
  109.1 49.5 %all-reduce.2.cloned.1.call-done = bf16[1,1024,1024]{2,1,0:T(8,128)(2,1)} async-done(((bf16[1,1024,1024]{2,1,0:T(8,128)(2,1)}), bf16[1,1024,1024]{2,1,0:T(8,128)(2,1)}) %all-reduce.2.cloned.1.call-update) | async-done | bytes 2097168 | tf_op jit(solution)/shard_map/psum | solution.py:24
  158.7 2.4 fusion
  161.8 0.0 copy-start
  161.9 0.0 copy-start.1
  161.9 9.9 %fusion.2 = f32[1024,1792]{1,0:T(8,128)} fusion(bf16[1,1024,1,1,1,1,1792]{6,1,5,4,3,2,0:T(8,128)(2,1)} %bitcast.2, pred[1024]{0:T(1024)(128)(4,1)S(1)} %iota_compare_fusion.1, bf16[1,1024,1024]{2,1,0:T(8,128)(2,1)} %all-reduce.2.cloned.1.call-done, f32[]{:T(128)} %bitcast.7), kind=kOutput, calls=%fused_computation.7 | convolution fusion | flops 3763077120 | bytes 13108228 | tf_op jit(solution)/shard_map/mcd,mdr->mcr/dot_general | solution.py:30
  171.7 0.0 copy-done
  171.7 10.1 %fusion.7 = bf16[1,1024,1792]{2,1,0:T(8,128)(2,1)S(1)} fusion(f32[1024,1792]{1,0:T(8,128)} %fusion.2, f32[]{:T(128)} %bitcast.6, f32[]{:T(128)S(6)} %mul.54, bf16[1024,1792]{1,0:T(8,128)(2,1)S(1)} %copy-done, bf16[1,1024,1024]{2,1,0:T(8,128)(2,1)S(1)} %copy-done.1, f32[]{:T(128)} %bitcast.7), kind=kOutput, calls=%fused_computation.14 | convolution fusion | flops 3781427200 | bytes 16777228 | tf_op jit(solution)/shard_map/mcd,mdr->mcr/dot_general | solution.py:33
  181.9 52.2 %copy.7 = bf16[1,1024,1792]{2,0,1:T(2,128)(2,1)} copy(bf16[1,1024,1792]{2,1,0:T(8,128)(2,1)S(1)} %fusion.7) | data formatting | bytes 7340032 | tf_op jit(solution)/shard_map/convert_element_type | solution.py:37
  234.1 0.6 broadcast.60
  234.7 38.7 %reduce.1 = bf16[1024,1792]{1,0:T(8,128)(2,1)} reduce(bf16[1024,1,1792]{2,1,0:T(2,128)(2,1)} %bitcast.27, bf16[]{:T(256)} %broadcast.60), dimensions={1}, to_apply=%bitcast.26.reduce_sub_computation | reduce | bytes 7340034
  273.3 6.6 %reshape.127 = bf16[8,2,114688]{2,1,0:T(2,128)(2,1)} reshape(bf16[1024,1792]{1,0:T(8,128)(2,1)} %reduce.1) | data formatting | bytes 7340032
  279.9 85.2 %all_to_all.27 = bf16[8,2,114688]{2,1,0:T(2,128)(2,1)} all-to-all(bf16[8,2,114688]{2,1,0:T(2,128)(2,1)} %reshape.127), channel_id=1, replica_groups=mesh['dp'=8,'owner'=4] {'dp'}, dimensions={0} | all-to-all | bytes 7340032 | tf_op jit(solution)/shard_map/all_to_all | solution.py:38
  365.2 8.3 %reshape.128 = bf16[1024,1,1792]{2,1,0:T(2,128)(2,1)} reshape(bf16[8,2,114688]{2,1,0:T(2,128)(2,1)} %all_to_all.27) | data formatting | bytes 7340032
  373.5 5.5 %copy.5 = bf16[1,1024,1792]{2,1,0:T(8,128)(2,1)} copy(bf16[1,1024,1792]{2,0,1:T(2,128)(2,1)} %bitcast.28) | data formatting | bytes 7340032
  (2 shorter events, 0.0 us)
Async XLA Ops:
  11.9 5.7 %copy-start.2 = (s32[8]{0:T(128)S(1)}, s32[8]{0:T(128)}, u32[]{:S(2)}) copy-start(s32[8]{0:T(128)} %param.3) | copy-start | bytes 100
  11.9 83.9 %all-to-all-start = ((bf16[8,128,1792]{2,1,0:T(8,128)(2,1)}), bf16[8,128,1792]{2,1,0:T(8,128)(2,1)}, u32[]{:S(2)}, u32[]{:S(2)}) async-start(bf16[8,128,1792]{2,1,0:T(8,128)(2,1)} %convert_element_type.32), calls=%async_computation | async-start | bytes 7340032 | tf_op jit(solution)/shard_map/all_to_all | solution.py:13
  17.6 141.1 %all-reduce.2.cloned.1.call-start = ((), (), s32[]{:S(2)}) async-start(), calls=%async_computation.2 | async-start | bytes 4194304 | tf_op jit(solution)/shard_map/psum | solution.py:24
  161.8 9.9 %copy-start = (bf16[1024,1792]{1,0:T(8,128)(2,1)S(1)}, bf16[1024,1792]{1,0:T(8,128)(2,1)}, u32[]{:S(2)}) copy-start(bf16[1024,1792]{1,0:T(8,128)(2,1)} %bitcast_select_fusion) | copy-start | bytes 11010052
  161.9 9.9 %copy-start.1 = (bf16[1,1024,1024]{2,1,0:T(8,128)(2,1)S(1)}, bf16[1,1024,1024]{2,1,0:T(8,128)(2,1)}, u32[]{:S(2)}) copy-start(bf16[1,1024,1024]{2,1,0:T(8,128)(2,1)} %all-reduce.2.cloned.1.call-done) | copy-start | bytes 6291460
Sparse Core Ops, SparseCore 0:
  104.4 54.1 all-reduce.1
where the time goes:
time: 391 us; the launch traced here: 386 us
  waiting for transfers between devices  126 us (32%)
  blocking collectives  85.2 us (22%)
  local copies, waits for them, and re-layouts  73.8 us (19%)
  other arithmetic  51.2 us (13%)
  matrix products  28.5 us (7%)
  between operations  14.8 us (4%)
  starting transfers between devices  5.71 us (1%)
    all_to_all x1, blocking collectives, body(): lax.all_to_all(update_rows, 'dp', split_axis=1, concat_axis=0, tiled=True)  85.2 us
    all_to_all x1, waiting for transfers between devices, body(): lax.all_to_all(narrowed, 'dp', split_axis=0, concat_axis=1, tiled=True)  76.9 us
    convert_element_type x1, local copies, waits for them, and re-layouts, body(): update_rows = (combined * (0.2 * math.sqrt(D))).astype(jnp.bfloat16)  52.2 us
    psum x1, waiting for transfers between devices, body(): lax.psum(partial_gram.astype(jnp.bfloat16), 'owner').astype(jnp.float32)  49.5 us
    unnamed x1, other arithmetic  38.7 us
    unnamed x10, local copies, waits for them, and re-layouts  21 us
    dot_general x1, matrix products, body(): jnp.einsum('mcd,mdr->mcr', normed_gram, once.astype(jnp.bfloat16), prefer...  10.1 us
    dot_general x1, matrix products, body(): jnp.einsum('mcd,mdr->mcr', normed_gram, regrouped, preferred_element_type...  9.87 us
  transfers between devices with their start and end apart: 2, of which 2 were waited for; matrix products, arithmetic and copies ran while one was open for 1% of the time, Pallas kernels for 0%

commit v1 on v0

v1 whole, which is shorter than its diff:
```python
import functools
import math

import jax
import jax.numpy as jnp
from jax import lax
from jax.experimental import pallas as pl
from jax.experimental.pallas import tpu as pltpu
from jax.sharding import PartitionSpec as P

MESH = pl.DeviceIdType.MESH
NT = (((1,), (1,)), ((), ()))
NN = (((1,), (0,)), ((), ()))


def flip(index, bits, count):
    out, bit = 0, 1
    while bit < count:
        out = out + bit * (((index // bit) % 2 + (bits // bit) % 2) % 2)
        bit *= 2
    return out


def kernel(
    n, owners, width_all, live_ref, grad_ref, out_ref,
    stage, send, rows, gram, normed, upd, part, got,
    load_sem, send_sem, recv_sem, psend_sem, precv_sem, usend_sem, urecv_sem, own_sem,
):
    d = lax.axis_index("dp")
    o = lax.axis_index("owner")
    size, width = stage.shape[1], stage.shape[2]
    hidden = rows.shape[0]
    strip = max(size, min(128, hidden))
    strips = hidden // strip
    per = strip // size
    levels = owners.bit_length() - 1

    def far_first(j):
        return 1 + (j + n // 2 - 1) % (n - 1)

    def load(slot):
        return pltpu.make_async_copy(grad_ref.at[flip(d, slot, n)], stage.at[slot], load_sem.at[slot])

    def forward(slot):
        return pltpu.make_async_remote_copy(
            src_ref=send.at[slot],
            dst_ref=rows.at[pl.ds(pl.multiple_of(slot * size, size), size)],
            send_sem=send_sem.at[slot],
            recv_sem=recv_sem.at[slot],
            device_id={"dp": flip(d, slot, n)},
            device_id_type=MESH,
        )

    def back(slot):
        return pltpu.make_async_remote_copy(
            src_ref=upd.at[pl.ds(pl.multiple_of(slot * size, size), size)],
            dst_ref=out_ref.at[d],
            send_sem=usend_sem.at[slot],
            recv_sem=urecv_sem.at[slot],
            device_id={"dp": flip(d, slot, n)},
            device_id_type=MESH,
        )

    def back_arrival(slot):
        return pltpu.make_async_remote_copy(
            src_ref=upd.at[pl.ds(pl.multiple_of(slot * size, size), size)],
            dst_ref=out_ref.at[flip(d, slot, n)],
            send_sem=usend_sem.at[slot],
            recv_sem=urecv_sem.at[slot],
            device_id={"dp": flip(d, slot, n)},
            device_id_type=MESH,
        )

    def share(level, s):
        cols = (s + 1) * strip
        return pltpu.make_async_remote_copy(
            src_ref=part.at[level, s, :, pl.ds(0, cols)],
            dst_ref=got.at[level, s, :, pl.ds(0, cols)],
            send_sem=psend_sem.at[level, s],
            recv_sem=precv_sem.at[level, s],
            device_id={"owner": flip(o, 2**level, owners)},
            device_id_type=MESH,
        )

    @pl.loop(0, n - 1)
    def _(j):
        load(far_first(j)).start()

    load(0).start()

    barrier = pltpu.get_barrier_semaphore()

    @pl.loop(1, n)
    def _(k):
        pl.semaphore_signal(barrier, inc=1, device_id={"dp": flip(d, k, n)}, device_id_type=MESH)

    for level in range(levels):
        pl.semaphore_signal(
            barrier, inc=1, device_id={"owner": flip(o, 2**level, owners)}, device_id_type=MESH
        )
    pl.semaphore_wait(barrier, n - 1 + levels)

    row_index = d * size + lax.broadcasted_iota(jnp.int32, (size, width), 0)

    def narrow(slot):
        load(slot).wait()
        live = live_ref[flip(d, slot, n)]
        return jnp.where(row_index < live, stage[slot], 0.0).astype(jnp.bfloat16)

    @pl.loop(0, n - 1)
    def _(j):
        slot = far_first(j)
        send[slot] = narrow(slot)
        forward(slot).start()

    rows[pl.ds(0, size), :] = narrow(0)

    eye = (
        lax.broadcasted_iota(jnp.int32, (strip, strip), 0)
        == lax.broadcasted_iota(jnp.int32, (strip, strip), 1)
    )
    trace = jnp.zeros((1, 1), jnp.float32)

    def settle(s, trace):
        at = s * strip
        cols = at + strip
        share(levels - 1, s).wait_recv()
        total = (
            part[levels - 1, s, :, 0:cols].astype(jnp.float32)
            + got[levels - 1, s, :, 0:cols].astype(jnp.float32)
        )
        gram[at:cols, 0:cols] = total
        for j in range(s):
            gram[j * strip : (j + 1) * strip, at:cols] = total[:, j * strip : (j + 1) * strip].T
        own = jnp.where(eye, total[:, at:cols], 0.0)
        return trace + jnp.sum(own, keepdims=True)

    for s in range(strips):
        cols = (s + 1) * strip
        if s == 0:
            @pl.loop(1, per)
            def _(k):
                forward(k).wait_recv()
        else:
            @pl.loop(s * per, (s + 1) * per)
            def _(k):
                forward(k).wait_recv()

        part[0, s, :, 0:cols] = lax.dot_general(
            rows[s * strip : cols, :], rows[0:cols, :], NT, preferred_element_type=jnp.float32
        ).astype(jnp.bfloat16)
        share(0, s).start()
        if s > 0:
            trace = settle(s - 1, trace)
        for level in range(1, levels):
            share(level - 1, s).wait_recv()
            part[level, s, :, 0:cols] = (
                part[level - 1, s, :, 0:cols].astype(jnp.float32)
                + got[level - 1, s, :, 0:cols].astype(jnp.float32)
            ).astype(jnp.bfloat16)
            share(level, s).start()
    trace = settle(strips - 1, trace)

    live_count = jnp.full((1, 1), live_ref[d], jnp.int32).astype(jnp.float32)
    scale_sq = 2.0 * trace / live_count
    shrink = 1.0 / scale_sq
    gain = (0.2 * math.sqrt(width_all)) / jnp.sqrt(scale_sq)

    @pl.loop(0, strips)
    def _(s):
        at = pl.ds(pl.multiple_of(s * strip, strip), strip)
        normed[at, :] = (gram[at, :] * shrink).astype(jnp.bfloat16)

    def update(s):
        at = pl.ds(pl.multiple_of(s * strip, strip), strip)
        square = lax.dot_general(normed[at, :], normed[...], NN, preferred_element_type=jnp.float32)
        mix = (2.0315 * square - 4.775 * normed[at, :].astype(jnp.float32)).astype(jnp.bfloat16)
        moved = lax.dot_general(mix, rows[...], NN, preferred_element_type=jnp.float32)
        upd[at, :] = ((3.4445 * rows[at, :].astype(jnp.float32) + moved) * gain).astype(jnp.bfloat16)

    if per == 1:
        @pl.loop(0, n - 1)
        def _(j):
            slot = far_first(j)
            update(slot)
            back(slot).start()

        update(0)
    else:
        @pl.loop(1, strips)
        def _(s):
            update(s)

            @pl.loop(0, per)
            def _(k):
                back(s * per + k).start()

        update(0)

        @pl.loop(1, per)
        def _(k):
            back(k).start()

    own_copy = pltpu.make_async_copy(upd.at[pl.ds(0, size)], out_ref.at[d], own_sem)
    own_copy.start()

    for s in range(strips):
        for level in range(levels):
            share(level, s).wait_send()

    @pl.loop(1, n)
    def _(k):
        forward(k).wait_send()

    @pl.loop(1, n)
    def _(k):
        back(k).wait_send()
        back_arrival(k).wait_recv()

    own_copy.wait()


def solution(mesh):
    n, owners = mesh.shape["dp"], mesh.shape["owner"]

    def body(gradients, rows_live):
        matrices, size, width = gradients.shape
        hidden = size * n
        strip = max(size, min(128, hidden))
        strips = hidden // strip
        levels = owners.bit_length() - 1
        dma = pltpu.SemaphoreType.DMA
        return pl.pallas_call(
            functools.partial(kernel, n, owners, width * owners),
            out_shape=jax.ShapeDtypeStruct((matrices, size, width), jnp.bfloat16),
            in_specs=[
                pl.BlockSpec(memory_space=pltpu.SMEM),
                pl.BlockSpec(memory_space=pl.ANY),
            ],
            out_specs=pl.BlockSpec(memory_space=pl.ANY),
            scratch_shapes=[
                pltpu.VMEM((n, size, width), jnp.float32),
                pltpu.VMEM((n, size, width), jnp.bfloat16),
                pltpu.VMEM((hidden, width), jnp.bfloat16),
                pltpu.VMEM((hidden, hidden), jnp.float32),
                pltpu.VMEM((hidden, hidden), jnp.bfloat16),
                pltpu.VMEM((hidden, width), jnp.bfloat16),
                pltpu.VMEM((levels, strips, strip, hidden), jnp.bfloat16),
                pltpu.VMEM((levels, strips, strip, hidden), jnp.bfloat16),
                dma((n,)), dma((n,)), dma((n,)),
                dma((levels, strips)), dma((levels, strips)),
                dma((n,)), dma((n,)), dma,
            ],
            compiler_params=pltpu.CompilerParams(
                collective_id=0, has_side_effects=True, vmem_limit_bytes=60 * 2**20
            ),
        )(rows_live, gradients)

    return jax.shard_map(
        body,
        mesh=mesh,
        in_specs=(P(None, "dp", "owner"), P()),
        out_specs=P(None, "dp", "owner"),
        check_vma=False,
    )
```

time: 391 us -> 182 us (0.47); the launches traced: 386 us -> 182 us
  Pallas kernels: 0 us -> 178 us
  waiting for transfers between devices: 126 us -> 0 us
  blocking collectives: 85.2 us -> 0 us
  local copies, waits for them, and re-layouts: 73.8 us -> 4.13 us
  other arithmetic: 51.2 us -> 0 us
  matrix products: 28.5 us -> 0 us
  between operations: 14.8 us -> 0.01 us
  starting transfers between devices: 5.71 us -> 0 us
    pallas_call x0 -> x1, Pallas kernels: none -> 178 us  [body(): pl.pallas_call(functools.partial(kernel, n, owners, width * owners), out_...]
    all_to_all x1 -> x0, blocking collectives: 85.2 us -> none  [body(): lax.all_to_all(update_rows, 'dp', split_axis=1, concat_axis=0, tiled=True)]
    all_to_all x1 -> x0, waiting for transfers between devices: 76.9 us -> none  [body(): lax.all_to_all(narrowed, 'dp', split_axis=0, concat_axis=1, tiled=True)]
    convert_element_type x1 -> x0, local copies, waits for them, and re-layouts: 52.2 us -> none  [body(): update_rows = (combined * (0.2 * math.sqrt(D))).astype(jnp.bfloat16)]
    psum x1 -> x0, waiting for transfers between devices: 49.5 us -> none  [body(): lax.psum(partial_gram.astype(jnp.bfloat16), 'owner').astype(jnp.float32)]
    unnamed x1 -> x0, other arithmetic: 38.7 us -> none
    dot_general x3 -> x0, matrix products: 28.5 us -> none  [the longest x1 10.1 us: body(): jnp.einsum('mcd,mdr->mcr', normed_gram, once.astype(jnp.bfloat16), prefer...]
    unnamed x10 -> x1, local copies, waits for them, and re-layouts: 21 us -> 4.13 us
  transfers between devices with their start and end apart: 2 -> 0, of which waited for: 2 -> 0; matrix products, arithmetic and copies ran while one was open for 1% -> 0% of each run, Pallas kernels for 0% -> 0%
where the time goes in v1:
time: 182 us
  Pallas kernels  178 us (98%)
  local copies, waits for them, and re-layouts  4.13 us (2%)
    pallas_call x1, Pallas kernels, body(): pl.pallas_call(functools.partial(kernel, n, owners, width * owners), out_...  178 us
    unnamed x1, local copies, waits for them, and re-layouts  4.13 us

profile of v1, /device:TPU:17, one launch (start us, length us, event | category | flops | bytes accessed | tf_op | source)
XLA Modules:
  0.0 182.2 jit_solution(16365998911488674156)
XLA Ops:
  0.0 178.0 %shard_map.28 = bf16[8,128,1792]{2,1,0:T(8,128)(2,1)} custom-call(s32[8]{0:T(128)} %live_ref.1, f32[8,128,1792]{2,1,0:T(8,128)} %grad_ref.1), custom_call_target="tpu_custom_call" | custom-call | tf_op jit(solution)/shard_map/pallas_call | solution.py:233
  178.0 4.1 %copy.4 = bf16[8,128,1792]{2,1,0:T(8,128)(2,1)} copy(bf16[8,128,1792]{2,1,0:T(8,128)(2,1)} %shard_map.28) | data formatting | bytes 7340032

commit v2 on v1

--- a/solution.py
+++ b/solution.py
@@ -35,8 +35,26 @@
     per = strip // size
     levels = owners.bit_length() - 1
 
-    def far_first(j):
-        return 1 + (j + n // 2 - 1) % (n - 1)
+    inner = ((d // (n // 2)) % 2 + (d // (n // 4)) % 2) % 2
+    to_inner = n // 2 + inner * (n // 4)
+    to_outer = n // 2 + (1 - inner) * (n // 4)
+
+    def each(start, count):
+        def over(fn):
+            @pl.loop(0, count)
+            def _(j):
+                fn(start + j)
+        return over
+
+    def gather_order(fn):
+        each(to_inner, n // 4)(fn)
+        each(1, n // 2 - 1)(fn)
+        each(to_outer, n // 4)(fn)
+
+    def return_order(fn):
+        each(to_outer, n // 4)(fn)
+        each(to_inner, n // 4)(fn)
+        each(1, n // 2 - 1)(fn)
 
     def load(slot):
         return pltpu.make_async_copy(grad_ref.at[flip(d, slot, n)], stage.at[slot], load_sem.at[slot])
@@ -82,10 +100,7 @@
             device_id_type=MESH,
         )
 
-    @pl.loop(0, n - 1)
-    def _(j):
-        load(far_first(j)).start()
-
+    gather_order(lambda slot: load(slot).start())
     load(0).start()
 
     barrier = pltpu.get_barrier_semaphore()
@@ -107,9 +122,8 @@
         live = live_ref[flip(d, slot, n)]
         return jnp.where(row_index < live, stage[slot], 0.0).astype(jnp.bfloat16)
 
-    @pl.loop(0, n - 1)
-    def _(j):
-        slot = far_first(j)
+    @gather_order
+    def _(slot):
         send[slot] = narrow(slot)
         forward(slot).start()
 
@@ -150,8 +164,8 @@
             rows[s * strip : cols, :], rows[0:cols, :], NT, preferred_element_type=jnp.float32
         ).astype(jnp.bfloat16)
         share(0, s).start()
-        if s > 0:
-            trace = settle(s - 1, trace)
+        if s > 1:
+            trace = settle(s - 2, trace)
         for level in range(1, levels):
             share(level - 1, s).wait_recv()
             part[level, s, :, 0:cols] = (
@@ -159,7 +173,8 @@
                 + got[level - 1, s, :, 0:cols].astype(jnp.float32)
             ).astype(jnp.bfloat16)
             share(level, s).start()
-    trace = settle(strips - 1, trace)
+    for s in range(max(strips - 2, 0), strips):
+        trace = settle(s, trace)
 
     live_count = jnp.full((1, 1), live_ref[d], jnp.int32).astype(jnp.float32)
     scale_sq = 2.0 * trace / live_count
@@ -179,9 +194,8 @@
         upd[at, :] = ((3.4445 * rows[at, :].astype(jnp.float32) + moved) * gain).astype(jnp.bfloat16)
 
     if per == 1:
-        @pl.loop(0, n - 1)
-        def _(j):
-            slot = far_first(j)
+        @return_order
+        def _(slot):
             update(slot)
             back(slot).start()
 

time: 182 us -> 185 us (1.016)
  Pallas kernels: 178 us -> 180 us
    pallas_call x1, Pallas kernels: 178 us -> 180 us  [body(): pl.pallas_call(functools.partial(kernel, n, owners, width * owners), out_...]
where the time goes in v2:
time: 185 us; the launch traced here: 184 us
  Pallas kernels  180 us (97%)
  local copies, waits for them, and re-layouts  4.13 us (2%)
    pallas_call x1, Pallas kernels, body(): pl.pallas_call(functools.partial(kernel, n, owners, width * owners), out_...  180 us
    unnamed x1, local copies, waits for them, and re-layouts  4.13 us

profile of v2, /device:TPU:17, one launch (start us, length us, event | category | flops | bytes accessed | tf_op | source)
XLA Modules:
  0.0 184.3 jit_solution(14742510187036713304)
XLA Ops:
  0.0 180.1 %shard_map.28 = bf16[8,128,1792]{2,1,0:T(8,128)(2,1)} custom-call(s32[8]{0:T(128)} %live_ref.1, f32[8,128,1792]{2,1,0:T(8,128)} %grad_ref.1), custom_call_target="tpu_custom_call" | custom-call | tf_op jit(solution)/shard_map/pallas_call | solution.py:247
  180.1 4.1 %copy.4 = bf16[8,128,1792]{2,1,0:T(8,128)(2,1)} copy(bf16[8,128,1792]{2,1,0:T(8,128)(2,1)} %shard_map.28) | data formatting | bytes 7340032
